TPU v7x, 32 devices: a whole 2x2x4 slice. The times are simulated.
32 devices in a mesh: groups: 1, role: 2 (over core), dev: 16 (over z, y, x).
Axes of the slice: x: 2, y: 2, z: 4, core: 2. Of those that a mesh axis runs over, the one named last changes fastest.
Arguments:
- prompt_hidden: bfloat16 [4096, 4096], P(('groups', 'dev')), may hold values from -6 to 6
- norm_gain: float32 [4096], replicated, may hold values from 0.25 to 1.75
- kv_weight: bfloat16 [4096, 4, 2, 128], P(None, 'role'), may hold values from -0.09375 to 0.09375
- prompt_excess: int32 [4], P('groups'), may hold values from 1 to 1536, 2048 in all
- prompt_owner: int32 [4], P('groups'), may hold values from 0 to 15, as said below
- response_counts: int32 [4], P('groups'), may hold values from 1 to 5, as said below
- queries: bfloat16 [256, 16, 128], P(('groups', 'dev'), 'role'), may hold values from -256 to 256
- new_kv: bfloat16 [256, 4, 2, 128], P(('groups', 'dev'), 'role'), may hold values from -6 to 6
- response_cache: bfloat16 [256, 256, 4, 2, 128], P(('groups', 'dev'), None, 'role'), may hold values from -6 to 6
- positions: int32 [256], P(('groups', 'dev')), may hold values from 0 to 256
- out_weight: bfloat16 [16, 128, 4096], P('role', None, 'dev'), may hold values from -0.125 to 0.125
Outputs:
- attended: bfloat16 [256, 16, 128], P(('groups', 'dev'), 'role')
- block_out: bfloat16 [256, 4096], P(('groups', 'role'), 'dev')
Inputs may be any that keep to these rules, and one draw needn't show every extreme that they name: `prompt_owner`: no device along dev owns more than two prompts, and some device owns exactly two. `response_counts`: some prompt has exactly 5 responses.
All inputs are finite; a program needn't handle non-finite values.
Results may differ from a plain program's by a relative error of at most 0.0065.
Values may be sent and summed in bfloat16 or wider, within the bound.
No kernel may reach another device: no remote copies, remote signals or barrier semaphores. Data moves between devices by JAX's collectives and lax.ppermute only.
A program may use at most 192 MiB of HBM per device.

v0:
```python
import jax
import jax.numpy as jnp
from jax import lax
from jax.sharding import PartitionSpec as P

RESP = 5
PROMPT_MIN = 512
rope_base = 500000.0


def merged_2(part, axis, combine):
    gathered = jax.tree.map(lambda a: lax.all_gather(a, axis), part)

    def take(source):
        return jax.tree.map(lambda a: lax.dynamic_index_in_dim(a, source, 0, False), gathered)

    return lax.fori_loop(
        1, lax.axis_size(axis), lambda source, state: combine(state, take(source)), take(0)
    )


def rotate(vectors, offsets):
    half = vectors.shape[-1] // 2
    freq = rope_base ** (-jnp.arange(half, dtype=jnp.float32) * 2.0 / vectors.shape[-1])
    angles = offsets.astype(jnp.float32)[:, None] * freq[None, :]
    cosine = jnp.cos(angles)[:, None, :]
    sine = jnp.sin(angles)[:, None, :]
    first = vectors[..., :half]
    second = vectors[..., half:]
    return jnp.concatenate(
        [first * cosine - second * sine, second * cosine + first * sine], axis=-1
    )


def prompt_layout(prompt_excess, token_index):
    lengths = PROMPT_MIN + prompt_excess
    ends = jnp.cumsum(lengths)
    starts = ends - lengths
    prompt_id = jnp.sum((token_index[:, None] >= ends[None, :]).astype(jnp.int32), axis=1)
    member = prompt_id[:, None] == jnp.arange(lengths.shape[0], dtype=jnp.int32)[None, :]
    offsets = token_index - jnp.sum(jnp.where(member, starts[None, :], 0), axis=1)
    return (member, offsets, starts, lengths)


def first_slots(owner, counts):
    order = jnp.arange(owner.shape[0], dtype=jnp.int32)
    earlier = (owner[:, None] == owner[None, :]) & (order[None, :] < order[:, None])
    return jnp.sum(jnp.where(earlier, counts[None, :], 0), axis=1)


def slot_prompts(owner, counts, slot_device, slot_index):
    order = jnp.arange(owner.shape[0], dtype=jnp.int32)
    first = first_slots(owner, counts)
    match = (
        (owner[None, :] == slot_device[:, None])
        & (first[None, :] <= slot_index[:, None])
        & (slot_index[:, None] < first[None, :] + counts[None, :])
    )
    present = jnp.any(match, axis=1)
    chosen = jnp.sum(jnp.where(match, order[None, :], 0), axis=1)
    return (chosen, present)


def softmax_state(scores, valid):
    scores = jnp.where(valid[:, None, None, :], scores, -1e30)
    peak = jnp.max(scores, axis=-1)
    weights = jnp.where(valid[:, None, None, :], jnp.exp(scores - peak[..., None]), 0.0)
    return (peak, jnp.sum(weights, axis=-1), weights.astype(jnp.bfloat16))


def state_each(query, keys, values, valid, scale):
    scores = jnp.einsum("sngd,slnd->sngl", query, keys, preferred_element_type=jnp.float32) * scale
    peak, total, rounded = softmax_state(scores, valid)
    mixed = jnp.einsum("sngl,slnd->sngd", rounded, values, preferred_element_type=jnp.float32)
    return (peak, total, mixed)


def state_shared(query, keys, values, valid, scale):
    scores = jnp.einsum("sngd,lnd->sngl", query, keys, preferred_element_type=jnp.float32) * scale
    peak, total, rounded = softmax_state(scores, valid)
    mixed = jnp.einsum("sngl,lnd->sngd", rounded, values, preferred_element_type=jnp.float32)
    return (peak, total, mixed)


def combine(first, second):
    peak = jnp.maximum(first[0], second[0])
    left_scale = jnp.exp(first[0] - peak)
    right_scale = jnp.exp(second[0] - peak)
    total = first[1] * left_scale + second[1] * right_scale
    mixed = first[2] * left_scale[..., None] + second[2] * right_scale[..., None]
    return (peak, total, mixed)


def on_device(
    prompt_hidden,
    norm_gain,
    kv_weight,
    prompt_excess,
    prompt_owner,
    response_counts,
    queries,
    new_kv,
    response_cache,
    positions,
    out_weight,
):
    device = lax.axis_index("dev")
    rows = prompt_hidden.shape[0]
    width = prompt_hidden.shape[1]
    local_heads = kv_weight.shape[1]
    head_size = kv_weight.shape[3]
    slots = queries.shape[0]
    query_heads = queries.shape[1]
    group = query_heads // local_heads
    prompt_count = prompt_excess.shape[0]
    scale = head_size ** (-0.5)
    token_index = device * rows + jnp.arange(rows, dtype=jnp.int32)
    member, offsets, starts, lengths = prompt_layout(prompt_excess, token_index)
    hidden = prompt_hidden.astype(jnp.float32)
    normed = (
        hidden * lax.rsqrt(jnp.mean(hidden * hidden, axis=-1, keepdims=True) + 1e-05) * norm_gain
    ).astype(jnp.bfloat16)
    projected = jnp.dot(
        normed,
        kv_weight.reshape(width, local_heads * 2 * head_size),
        preferred_element_type=jnp.float32,
    )
    projected = projected.reshape(rows, local_heads, 2, head_size)
    prompt_keys = rotate(projected[:, :, 0], offsets).astype(jnp.bfloat16)
    prompt_values = projected[:, :, 1].astype(jnp.bfloat16)
    grouped = queries.reshape(slots, local_heads, group, head_size)
    slot_index = jnp.arange(slots, dtype=jnp.int32)
    chosen, present = slot_prompts(
        prompt_owner, response_counts, jnp.zeros((slots,), jnp.int32) + device, slot_index
    )
    cache_valid = jnp.arange(response_cache.shape[1], dtype=jnp.int32)[None, :] < positions[:, None]
    cache_state = state_each(
        grouped, response_cache[:, :, :, 0], response_cache[:, :, :, 1], cache_valid, scale
    )
    self_valid = jnp.ones((slots, 1), dtype=bool)
    self_state = state_each(
        grouped, new_kv[:, None, :, 0], new_kv[:, None, :, 1], self_valid, scale
    )
    first = first_slots(prompt_owner, response_counts)
    rank = jnp.clip(slot_index - first[chosen], 0, RESP - 1)
    entry = chosen * RESP + rank
    select = (
        (entry[None, :] == jnp.arange(prompt_count * RESP, dtype=jnp.int32)[:, None])
        & present[None, :]
    ).astype(jnp.float32)
    table = jnp.dot(
        select,
        queries.reshape(slots, query_heads * head_size).astype(jnp.float32),
        precision=lax.Precision.HIGHEST,
    )
    table = lax.psum(table, "dev").astype(jnp.bfloat16)
    table = table.reshape(prompt_count, RESP, local_heads, group, head_size)
    held = jnp.any(member, axis=0)
    first_prompt = jnp.sum((starts + lengths <= token_index[0]).astype(jnp.int32))
    reach = min(rows // PROMPT_MIN + 2, prompt_count)
    layout = (
        jnp.full((prompt_count, RESP, local_heads, group), -1e30, jnp.float32),
        jnp.zeros((prompt_count, RESP, local_heads, group), jnp.float32),
        jnp.zeros((prompt_count, RESP, local_heads, group, head_size), jnp.float32),
    )
    for step in range(reach):
        pick = jnp.minimum(first_prompt + step, prompt_count - 1)
        live = (first_prompt + step < prompt_count) & held[pick]
        reply_queries = lax.dynamic_index_in_dim(table, pick, 0, keepdims=False)
        reply_live = jnp.arange(RESP, dtype=jnp.int32) < response_counts[pick]
        row_member = (token_index >= starts[pick]) & (token_index < starts[pick] + lengths[pick])
        valid = live & reply_live[:, None] & row_member[None, :]
        fresh = state_shared(reply_queries, prompt_keys, prompt_values, valid, scale)
        earlier = tuple(
            (lax.dynamic_index_in_dim(part_now, pick, 0, keepdims=False) for part_now in layout)
        )
        merged = combine(earlier, fresh)
        layout = tuple(
            (
                lax.dynamic_update_index_in_dim(part_now, part_new, pick, 0)
                for part_now, part_new in zip(layout, merged)
            )
        )
    joined_peak, joined_total, joined_mixed = merged_2(layout, "dev", combine)
    flat_peak = joined_peak.reshape(prompt_count * RESP, local_heads, group)
    flat_total = joined_total.reshape(prompt_count * RESP, local_heads, group)
    flat_mixed = joined_mixed.reshape(prompt_count * RESP, local_heads, group, head_size)
    own_peak = jnp.take(flat_peak, entry, axis=0)
    own_total = jnp.take(flat_total, entry, axis=0)
    own_mixed = jnp.take(flat_mixed, entry, axis=0)
    prompt_state = (
        jnp.where(present[:, None, None], own_peak, -1e30),
        jnp.where(present[:, None, None], own_total, 0.0),
        jnp.where(present[:, None, None, None], own_mixed, 0.0),
    )
    final = combine(combine(prompt_state, cache_state), self_state)
    attended = (
        (final[2] / final[1][..., None]).reshape(slots, query_heads, head_size).astype(jnp.bfloat16)
    )
    flat = attended.reshape(slots, query_heads * head_size)
    weight_flat = out_weight.reshape(query_heads * head_size, out_weight.shape[2])
    head_terms = jnp.dot(
        lax.all_gather(flat, "dev", axis=0, tiled=True),
        weight_flat,
        preferred_element_type=jnp.float32,
    )
    block_out = lax.psum_scatter(head_terms, "role", scatter_dimension=0, tiled=True).astype(
        jnp.bfloat16
    )
    return (attended, block_out)


def solution(mesh):
    return jax.shard_map(
        on_device,
        mesh=mesh,
        in_specs=(
            P(("groups", "dev"), None),
            P(),
            P(None, "role", None, None),
            P("groups"),
            P("groups"),
            P("groups"),
            P(("groups", "dev"), "role", None),
            P(("groups", "dev"), "role", None, None),
            P(("groups", "dev"), None, "role", None, None),
            P(("groups", "dev")),
            P("role", None, "dev"),
        ),
        out_specs=(P(("groups", "dev"), "role", None), P(("groups", "role"), "dev")),
        check_vma=False,
    )
```

profile of v0, /device:TPU:0, one launch (start us, length us, event | category | flops | bytes accessed | tf_op | source)
XLA Modules:
  0.0 298.8 jit_solution(10407446676272909244)
XLA Ops:
  8.6 1.9 bitcast_subtract_fusion.3
  13.4 1.3 fusion.107
  19.9 79.5 %psum.7 = bf16[20,1024]{1,0:T(8,128)(2,1)S(1)} all-reduce(f32[20,1024]{1,0:T(8,128)S(1)} %fusion.46), channel_id=1, replica_groups=mesh['groups'=1,'role'=2,'dev'=16] {'dev'}, use_global_device_ids=true, to_apply=%region_9.10 | all-reduce | flops 20480 | bytes 122880 | tf_op jit(solution)/shard_map/psum | solution.py:156
  99.5 7.2 %reshape.412 = bf16[4096,512]{1,0:T(8,128)(2,1)} reshape(bf16[4096,2,2,128]{3,2,1,0:T(2,128)(2,1)} %param.17) | data formatting | bytes 8388608 | tf_op jit(solution)/shard_map/reshape | solution.py:125
  106.7 6.6 %copy.138 = bf16[512,4096]{1,0:T(8,128)(2,1)} copy(bf16[512,4096]{0,1:T(8,128)(2,1)} %bitcast.222) | data formatting | bytes 8388608 | tf_op jit(solution)/shard_map/dot_general | solution.py:123
  113.8 3.6 %fusion.7 = f32[256,2,2,128]{0,3,2,1:T(8,128)S(1)} fusion(bf16[2,2,128,4096]{3,2,1,0:T(8,128)(2,1)} %bitcast.223, bf16[256,4096]{1,0:T(8,128)(2,1)S(1)} %copy-done.1, f32[4096]{0:T(1024)S(1)} %copy-done.7, f32[256]{0:T(256)S(1)} %add_rsqrt_fusion), kind=kOutput, calls=%fused_computation.18 | convolution fusion | flops 1077936128 | bytes 6833152 | tf_op jit(solution)/shard_map/dot_general | solution.py:123
  119.9 1.2 compare_and_fusion
  126.0 10.2 %fusion.106 = (bf16[16,256,2,1,128]{4,3,2,1,0:T(2,128)(2,1)}, bf16[16,256,2,1,128]{4,3,2,1,0:T(2,128)(2,1)}) fusion(bf16[16,256,2,2,128]{4,3,2,1,0:T(2,128)(2,1)} %param.23), kind=kLoop, calls=%fused_computation.189 | loop fusion | bytes 8388608 | tf_op jit(solution)/shard_map/slice | solution.py:138
  136.3 2.9 fusion.111
  140.1 37.8 %all_gather.32 = f32[16,4,5,2,4]{2,4,3,1,0:T(4,128)S(1)} all-gather(f32[1,4,5,2,4]{2,4,3,1,0:T(4,128)S(1)} %get-tuple-element.219), channel_id=1, replica_groups=mesh['groups'=1,'role'=2,'dev'=16] {'dev'}, dimensions={0}, use_global_device_ids=true | all-gather | bytes 10880 | tf_op jit(solution)/shard_map/all_gather | solution.py:12
  177.9 38.5 %all_gather.29 = f32[16,4,5,2,4]{2,4,3,1,0:T(4,128)S(1)} all-gather(f32[1,4,5,2,4]{2,4,3,1,0:T(4,128)S(1)} %get-tuple-element.220), channel_id=1, replica_groups=mesh['groups'=1,'role'=2,'dev'=16] {'dev'}, dimensions={0}, use_global_device_ids=true | all-gather | bytes 10880 | tf_op jit(solution)/shard_map/all_gather | solution.py:12
  217.4 22.4 %while.19 = (s32[]{:T(128)}, f32[4,5,2,4]{1,3,2,0:T(4,128)S(1)}, f32[4,5,2,4]{1,3,2,0:T(4,128)S(1)}, f32[4,5,2,4,128]{4,3,2,1,0:T(4,128)S(1)}, f32[16,4,5,2,4]{2...) while((s32[]{:T(128)}, f32[4,5,2,4]{1,3,2,0:T(4,128)S(1)}, ...), condition=%wide.region_15.16_spmd, body=%wide.region_14.15_spmd.sunk | while | flops 62405 | bytes 254871 | solution.py:17
  217.7 1.2 fusion.123
  219.2 1.2 fusion.123
  220.7 1.2 fusion.123
  222.2 1.2 fusion.123
  223.7 1.2 fusion.123
  225.2 1.2 fusion.123
  226.7 1.2 fusion.123
  228.2 1.2 fusion.123
  229.7 1.2 fusion.123
  231.2 1.2 fusion.123
  232.7 1.2 fusion.123
  234.2 1.2 fusion.123
  235.7 1.2 fusion.123
  237.2 1.2 fusion.123
  238.7 1.2 fusion.123
  242.7 2.7 fusion.24
  245.4 38.6 %all_gather.36 = bf16[256,1024]{1,0:T(8,128)(2,1)S(1)} all-gather(bf16[16,1024]{1,0:T(8,128)(2,1)S(1)} %convert_element_type.68), channel_id=1, replica_groups=mesh['groups'=1,'role'=2,'dev'=16] {'dev'}, dimensions={0}, use_global_device_ids=true | all-gather | bytes 557056 | tf_op jit(solution)/shard_map/all_gather | solution.py:203
  284.0 1.0 fusion.114
  285.1 5.3 %reduce-scatter.2.cloned.1.call-done = f32[128,256]{1,0:T(8,128)} async-done(((f32[256,256]{1,0:T(8,128)}), f32[128,256]{1,0:T(8,128)}) %reduce-scatter.2.cloned.1.call-update) | async-done | bytes 131088 | tf_op jit(solution)/shard_map/reduce_scatter | solution.py:207
  290.4 1.5 convert_element_type.69
  (148 shorter events, 21.0 us)
Async XLA Ops:
  7.2 276.9 %copy-start = (bf16[8,128,256]{2,1,0:T(8,128)(2,1)S(1)}, bf16[8,128,256]{2,1,0:T(8,128)(2,1)}, u32[]{:S(2)}) copy-start(bf16[8,128,256]{2,1,0:T(8,128)(2,1)} %param.25) | copy-start | bytes 1572868
  7.2 209.3 %all-gather.2.cloned.1.call-start = ((), (), s32[]{:S(2)}) async-start(), calls=%async_computation.1 | async-start | bytes 1392640 | tf_op jit(solution)/shard_map/all_gather | solution.py:12
  106.7 6.6 %copy-start.1 = (bf16[256,4096]{1,0:T(8,128)(2,1)S(1)}, bf16[256,4096]{1,0:T(8,128)(2,1)}, u32[]{:S(2)}) copy-start(bf16[256,4096]{1,0:T(8,128)(2,1)} %param.15) | copy-start | bytes 6291460
  106.7 7.1 %copy-start.7 = (f32[4096]{0:T(1024)S(1)}, f32[4096]{0:T(1024)}, u32[]{:S(2)}) copy-start(f32[4096]{0:T(1024)} %param.16) | copy-start | bytes 49156
  125.3 0.6 copy-start.2
  125.9 10.3 %copy-start.6 = (s32[16]{0:T(128)S(1)}, s32[16]{0:T(128)}, u32[]{:S(2)}) copy-start(s32[16]{0:T(128)} %param.24) | copy-start | bytes 196
  125.9 10.3 %copy-start.5 = (bf16[16,8,128]{2,1,0:T(8,128)(2,1)S(1)}, bf16[16,8,128]{2,1,0:T(8,128)(2,1)}, u32[]{:S(2)}) copy-start(bf16[16,8,128]{2,1,0:T(8,128)(2,1)} %param.21) | copy-start | bytes 98308
  126.0 13.4 %copy-start.3 = (bf16[16,2,2,128]{3,2,1,0:T(2,128)(2,1)S(1)}, bf16[16,2,2,128]{3,2,1,0:T(2,128)(2,1)}, u32[]{:S(2)}) copy-start(bf16[16,2,2,128]{3,2,1,0:T(2,128)(2,1)} %param.22) | copy-start | bytes 49156
  126.0 164.4 %reduce-scatter.2.cloned.1.call-start = ((), (), s32[]{:S(2)}) async-start(), calls=%async_computation.2 | async-start | bytes 393216 | tf_op jit(solution)/shard_map/reduce_scatter | solution.py:207
  245.4 46.5 %copy-start.4 = (bf16[16,2,4,128]{3,2,1,0:T(4,128)(2,1)}, bf16[16,2,4,128]{3,2,1,0:T(4,128)(2,1)S(1)}, u32[]{:S(2)}) copy-start(bf16[16,2,4,128]{3,2,1,0:T(4,128)(2,1)S(1)} %fusion.24) | copy-start | bytes 98308
Sparse Core Ops, SparseCore 0:
  126.1 53.9 all-gather.1
  285.2 5.1 reduce-scatter.1
where the time goes:
time: 300 us; the launch traced here: 299 us
  blocking collectives  194 us (65%)
  local copies, waits for them, and re-layouts  37.2 us (12%)
  other arithmetic  29.3 us (10%)
  between operations  20.1 us (7%)
  matrix products  12 us (4%)
  waiting for transfers between devices  5.37 us (2%)
    psum x1, blocking collectives, on_device(): table = lax.psum(table, 'dev').astype(jnp.bfloat16)  79.5 us
    all_gather x2, blocking collectives, merged_2(): gathered = jax.tree.map(lambda a: lax.all_gather(a, axis), part)  76.3 us
    all_gather x1, blocking collectives, on_device(): lax.all_gather(flat, 'dev', axis=0, tiled=True)  38.6 us
    add x15, other arithmetic, combine(): first[2] * left_scale[..., None] + second[2] * right_scale[..., None]  17.5 us
    slice x1, local copies, waits for them, and re-layouts, on_device(): response_cache[:, :, :, 0]  10.2 us
    reshape x1, local copies, waits for them, and re-layouts, on_device(): kv_weight.reshape(width, local_heads * 2 * head_size)  7.22 us
    dot_general x1, local copies, waits for them, and re-layouts, on_device(): jnp.dot(normed, kv_weight.reshape(width, local_heads * 2 * head_size), pr...  6.6 us
  transfers between devices with their start and end apart: 2, of which 1 were waited for; matrix products, arithmetic and copies ran while one was open for 5% of the time, Pallas kernels for 0%

commit v1 on v0

--- a/solution.py
+++ b/solution.py
@@ -153,7 +153,7 @@
         queries.reshape(slots, query_heads * head_size).astype(jnp.float32),
         precision=lax.Precision.HIGHEST,
     )
-    table = lax.psum(table, "dev").astype(jnp.bfloat16)
+    table = jnp.sum(lax.all_gather(table, "dev"), axis=0).astype(jnp.bfloat16)
     table = table.reshape(prompt_count, RESP, local_heads, group, head_size)
     held = jnp.any(member, axis=0)
     first_prompt = jnp.sum((starts + lengths <= token_index[0]).astype(jnp.int32))

time: 300 us -> 241 us (0.80)
  blocking collectives: 194 us -> 118 us
  waiting for transfers between devices: 5.37 us -> 24.1 us
  local copies, waits for them, and re-layouts: 37.2 us -> 34 us
    psum x1 -> x0, blocking collectives: 79.5 us -> none  [on_device(): table = lax.psum(table, 'dev').astype(jnp.bfloat16)]
    all_gather x0 -> x1, waiting for transfers between devices: none -> 20.3 us  [on_device(): table = jnp.sum(lax.all_gather(table, 'dev'), axis=0).astype(jnp.bfloat16)]
    slice x1, local copies, waits for them, and re-layouts: 10.2 us -> 6.99 us  [on_device(): response_cache[:, :, :, 0]]
  transfers between devices with their start and end apart: 2 -> 3, of which waited for: 1 -> 2; matrix products, arithmetic and copies ran while one was open for 5% -> 16% of each run, Pallas kernels for 0% -> 0%
where the time goes in v1:
time: 241 us; the launch traced here: 240 us
  blocking collectives  118 us (49%)
  local copies, waits for them, and re-layouts  34 us (14%)
  other arithmetic  30.8 us (13%)
  waiting for transfers between devices  24.1 us (10%)
  between operations  19.8 us (8%)
  matrix products  12.8 us (5%)
    all_gather x2, blocking collectives, merged_2(): gathered = jax.tree.map(lambda a: lax.all_gather(a, axis), part)  77.4 us
    all_gather x1, blocking collectives, on_device(): lax.all_gather(flat, 'dev', axis=0, tiled=True)  40.4 us
    all_gather x1, waiting for transfers between devices, on_device(): table = jnp.sum(lax.all_gather(table, 'dev'), axis=0).astype(jnp.bfloat16)  20.3 us
    add x15, other arithmetic, combine(): first[2] * left_scale[..., None] + second[2] * right_scale[..., None]  17.5 us
    reshape x1, local copies, waits for them, and re-layouts, on_device(): kv_weight.reshape(width, local_heads * 2 * head_size)  7.24 us
    slice x1, local copies, waits for them, and re-layouts, on_device(): response_cache[:, :, :, 0]  6.99 us
    dot_general x1, local copies, waits for them, and re-layouts, on_device(): jnp.dot(normed, kv_weight.reshape(width, local_heads * 2 * head_size), pr...  6.57 us
  transfers between devices with their start and end apart: 3, of which 2 were waited for; matrix products, arithmetic and copies ran while one was open for 16% of the time, Pallas kernels for 0%

profile of v1, /device:TPU:0, one launch (start us, length us, event | category | flops | bytes accessed | tf_op | source)
XLA Modules:
  0.0 239.8 jit_solution(860674896109455141)
XLA Ops:
  10.3 1.5 convolution_bitcast_fusion
  13.2 1.9 bitcast_subtract_fusion.3
  16.5 1.3 fusion.106
  20.6 7.2 %reshape.412 = bf16[4096,512]{1,0:T(8,128)(2,1)} reshape(bf16[4096,2,2,128]{3,2,1,0:T(2,128)(2,1)} %param.17) | data formatting | bytes 8388608 | tf_op jit(solution)/shard_map/reshape | solution.py:125
  27.9 6.6 %copy.136 = bf16[512,4096]{1,0:T(8,128)(2,1)} copy(bf16[512,4096]{0,1:T(8,128)(2,1)} %bitcast.224) | data formatting | bytes 8388608 | tf_op jit(solution)/shard_map/dot_general | solution.py:123
  37.4 1.2 compare_and_fusion
  41.5 3.7 %fusion.7 = f32[256,2,2,128]{0,3,2,1:T(8,128)S(1)} fusion(bf16[2,2,128,4096]{3,2,1,0:T(8,128)(2,1)} %bitcast.225, bf16[256,4096]{1,0:T(8,128)(2,1)S(1)} %copy-done.2, f32[4096]{0:T(1024)S(1)} %copy-done.8, f32[256]{0:T(256)S(1)} %add_rsqrt_fusion), kind=kOutput, calls=%fused_computation.18 | convolution fusion | flops 1077936128 | bytes 6833152 | tf_op jit(solution)/shard_map/dot_general | solution.py:123
  45.4 7.0 %fusion.105 = (bf16[16,256,2,1,128]{4,3,2,1,0:T(2,128)(2,1)}, bf16[16,256,2,1,128]{4,3,2,1,0:T(2,128)(2,1)}) fusion(bf16[16,256,2,2,128]{4,3,2,1,0:T(2,128)(2,1)S(1)} %copy-done.1), kind=kLoop, calls=%fused_computation.189 | loop fusion | bytes 8388608 | tf_op jit(solution)/shard_map/slice | solution.py:138
  52.3 20.3 %all-gather.7.cloned.1.call-done = f32[16,20,1024]{2,1,0:T(8,128)} async-done(((f32[1,20,1024]{2,1,0:T(8,128)}), f32[16,20,1024]{2,1,0:T(8,128)}) %all-gather.7.cloned.1.call-update) | async-done | bytes 1310736 | tf_op jit(solution)/shard_map/all_gather | solution.py:156
  72.7 1.5 reduce_sum.111
  76.2 2.9 %fusion.110 = (f32[16,2,4]{2,1,0:T(2,128)S(1)}, f32[16,2,4,256]{3,2,1,0:T(4,128)S(1)}) fusion(bf16[16,2,4,128]{3,2,1,0:T(4,128)(2,1)S(1)} %bitcast.234, bf16[16,256,2,1,128]{4,3,2,1,0:T(2,128)(2,1)} %get-tuple-element.211, pred[16,256]{1,0:T(8,128)(4,1)S(1)} %iota_compare_fusion), kind=kOutput, calls=%fused_computation.194 | convolution fusion | flops 8486784 | bytes 2265600 | tf_op jit(solution)/shard_map/sngd,slnd->sngl/dot_general | solution.py:72
  80.2 40.4 %all_gather.40 = f32[16,4,5,2,4]{2,4,3,1,0:T(4,128)S(1)} all-gather(f32[1,4,5,2,4]{2,4,3,1,0:T(4,128)S(1)} %get-tuple-element.219), channel_id=1, replica_groups=mesh['groups'=1,'role'=2,'dev'=16] {'dev'}, dimensions={0}, use_global_device_ids=true | all-gather | bytes 10880 | tf_op jit(solution)/shard_map/all_gather | solution.py:12
  120.5 37.1 %all_gather.37 = f32[16,4,5,2,4]{2,4,3,1,0:T(4,128)S(1)} all-gather(f32[1,4,5,2,4]{2,4,3,1,0:T(4,128)S(1)} %get-tuple-element.220), channel_id=1, replica_groups=mesh['groups'=1,'role'=2,'dev'=16] {'dev'}, dimensions={0}, use_global_device_ids=true | all-gather | bytes 10880 | tf_op jit(solution)/shard_map/all_gather | solution.py:12
  158.5 22.4 %while.19 = (s32[]{:T(128)}, f32[4,5,2,4]{1,3,2,0:T(4,128)S(1)}, f32[4,5,2,4]{1,3,2,0:T(4,128)S(1)}, f32[4,5,2,4,128]{4,3,2,1,0:T(4,128)S(1)}, f32[16,4,5,2,4]{2...) while((s32[]{:T(128)}, f32[4,5,2,4]{1,3,2,0:T(4,128)S(1)}, ...), condition=%wide.region_15.16_spmd, body=%wide.region_14.15_spmd.sunk | while | flops 62405 | bytes 254871 | solution.py:17
  158.8 1.2 fusion.122
  160.3 1.2 fusion.122
  161.8 1.2 fusion.122
  163.3 1.2 fusion.122
  164.8 1.2 fusion.122
  166.3 1.2 fusion.122
  167.8 1.2 fusion.122
  169.3 1.2 fusion.122
  170.8 1.2 fusion.122
  172.3 1.2 fusion.122
  173.8 1.2 fusion.122
  175.2 1.2 fusion.122
  176.7 1.2 fusion.122
  178.2 1.2 fusion.122
  183.8 2.7 %fusion.24 = bf16[16,2,4,128]{3,2,1,0:T(4,128)(2,1)S(1)} fusion(bf16[16,256,2,1,128]{4,3,2,1,0:T(2,128)(2,1)} %get-tuple-element.212, f32[16,2,4,256]{3,2,1,0:T(4,128)S(1)} %get-tuple-element.244, f32[16,2,4]{2,1,0:T(2,128)S(1)} %get-tuple-element.243, f32[16,2,4,128]{3,2,1,0:T(4,128)S(1)} %gather_fusion.1, pred[16,256]{1,0:T(8,128)(4,1)S(1)} %iota_compare_fusion, ...), kind=kOutput, calls=%fused_computation.39 | convolution fusion | flops 8667136 | bytes 2350624 | tf_op jit(solution)/shard_map/sngl,slnd->sngd/dot_general | solution.py:74
  186.5 40.4 %all_gather.44 = bf16[256,1024]{1,0:T(8,128)(2,1)S(1)} all-gather(bf16[16,1024]{1,0:T(8,128)(2,1)S(1)} %convert_element_type.73), channel_id=1, replica_groups=mesh['groups'=1,'role'=2,'dev'=16] {'dev'}, dimensions={0}, use_global_device_ids=true | all-gather | bytes 557056 | tf_op jit(solution)/shard_map/all_gather | solution.py:203
  228.0 3.8 %reduce-scatter.2.cloned.1.call-done = f32[128,256]{1,0:T(8,128)} async-done(((f32[256,256]{1,0:T(8,128)}), f32[128,256]{1,0:T(8,128)}) %reduce-scatter.2.cloned.1.call-update) | async-done | bytes 131088 | tf_op jit(solution)/shard_map/reduce_scatter | solution.py:207
  231.7 1.5 convert_element_type.74
  (153 shorter events, 22.3 us)
Async XLA Ops:
  7.2 219.8 %copy-start = (bf16[8,128,256]{2,1,0:T(8,128)(2,1)S(1)}, bf16[8,128,256]{2,1,0:T(8,128)(2,1)}, u32[]{:S(2)}) copy-start(bf16[8,128,256]{2,1,0:T(8,128)(2,1)} %param.25) | copy-start | bytes 1572868
  7.2 65.5 %all-gather.7.cloned.1.call-start = ((), (), s32[]{:S(2)}) async-start(), calls=%async_computation.3 | async-start | bytes 1671168 | tf_op jit(solution)/shard_map/all_gather | solution.py:156
  11.8 145.8 %all-gather.5.cloned.1.call-start = ((), (), s32[]{:S(2)}) async-start(), calls=%async_computation.1 | async-start | bytes 1392640 | tf_op jit(solution)/shard_map/all_gather | solution.py:12
  27.9 6.6 %copy-start.2 = (bf16[256,4096]{1,0:T(8,128)(2,1)S(1)}, bf16[256,4096]{1,0:T(8,128)(2,1)}, u32[]{:S(2)}) copy-start(bf16[256,4096]{1,0:T(8,128)(2,1)} %param.15) | copy-start | bytes 6291460
  27.9 13.7 %copy-start.8 = (f32[4096]{0:T(1024)S(1)}, f32[4096]{0:T(1024)}, u32[]{:S(2)}) copy-start(f32[4096]{0:T(1024)} %param.16) | copy-start | bytes 49156
  41.5 3.8 %copy-start.1 = (bf16[16,256,2,2,128]{4,3,2,1,0:T(2,128)(2,1)S(1)}, bf16[16,256,2,2,128]{4,3,2,1,0:T(2,128)(2,1)}, u32[]{:S(2)}) copy-start(bf16[16,256,2,2,128]{4,3,2,1,0:T(2,128)(2,1)} %param.23) | copy-start | bytes 12582916
  45.3 30.8 %copy-start.7 = (s32[16]{0:T(128)S(1)}, s32[16]{0:T(128)}, u32[]{:S(2)}) copy-start(s32[16]{0:T(128)} %param.24) | copy-start | bytes 196
  45.3 30.9 %copy-start.6 = (bf16[16,8,128]{2,1,0:T(8,128)(2,1)S(1)}, bf16[16,8,128]{2,1,0:T(8,128)(2,1)}, u32[]{:S(2)}) copy-start(bf16[16,8,128]{2,1,0:T(8,128)(2,1)} %param.21) | copy-start | bytes 98308
  52.3 26.9 %copy-start.4 = (bf16[16,2,2,128]{3,2,1,0:T(2,128)(2,1)S(1)}, bf16[16,2,2,128]{3,2,1,0:T(2,128)(2,1)}, u32[]{:S(2)}) copy-start(bf16[16,2,2,128]{3,2,1,0:T(2,128)(2,1)} %param.22) | copy-start | bytes 49156
  75.4 0.6 copy-start.3
  76.1 155.6 %reduce-scatter.2.cloned.1.call-start = ((), (), s32[]{:S(2)}) async-start(), calls=%async_computation.2 | async-start | bytes 393216 | tf_op jit(solution)/shard_map/reduce_scatter | solution.py:207
  186.5 46.8 %copy-start.5 = (bf16[16,2,4,128]{3,2,1,0:T(4,128)(2,1)}, bf16[16,2,4,128]{3,2,1,0:T(4,128)(2,1)S(1)}, u32[]{:S(2)}) copy-start(bf16[16,2,4,128]{3,2,1,0:T(4,128)(2,1)S(1)} %fusion.24) | copy-start | bytes 98308
Sparse Core Ops, SparseCore 0:
  11.9 60.6 all-gather.6
  76.2 56.6 all-gather.4
  228.1 3.5 reduce-scatter.1
